TPU v7x, 32 devices: a whole 2x2x4 slice. The times are simulated.
32 devices in a mesh: pipe: 8 (over z, y), tensor: 4 (over x, core).
Axes of the slice: x: 2, y: 2, z: 4, core: 2. Of those that a mesh axis runs over, the one named last changes fastest.
Arguments:
- memory: bfloat16 [2, 512, 4096], P(None, 'pipe', 'tensor'), may hold values from -6 to 6
- states: bfloat16 [8, 2, 256, 4096], P('pipe', None, None, 'tensor'), may hold values from -6 to 6
- norm_gain: float32 [8, 4096], P('pipe'), may hold values from 0.25 to 1.75
- w_query: bfloat16 [8, 4096, 4096], P('pipe', None, 'tensor'), may hold values from -0.09375 to 0.09375
- w_keyvalue: bfloat16 [8, 4096, 2, 4096], P('pipe', None, None, 'tensor'), may hold values from -0.09375 to 0.09375
- w_output: bfloat16 [8, 4096, 4096], P('pipe', 'tensor'), may hold values from -0.125 to 0.125
Outputs:
- updated: bfloat16 [8, 2, 256, 4096], P('pipe', None, None, 'tensor')
All inputs are finite; a program needn't handle non-finite values.
Results may differ from a plain program's by a relative error of at most 0.006.
Values may be sent and summed in bfloat16 or wider, within the bound.
A program may use at most 128 MiB of HBM per device.

v0:
```python
import functools

import jax
import jax.numpy as jnp
from jax import lax
from jax.experimental import pallas as pl
from jax.experimental.pallas import tpu as pltpu
from jax.sharding import PartitionSpec as P

HEAD_DIM = 64
CORES = 2
LOW = 2
TILE = 256
MAX_COPIES = 100
LANES = 128
SUB = 16
CHUNK = 256
MESH = pl.DeviceIdType.MESH
F32 = jnp.float32
BF16 = jnp.bfloat16


def copies_per_sequence(n_pipe, n_tensor):
    xs, highs = n_tensor // CORES, n_pipe // LOW
    return 4 * n_pipe * xs + (xs - 1) * highs


def kernel(
    n_pipe, n_tensor,
    mem_hbm, st_hbm, gain_ref, wq_hbm, wkv_hbm, wo_hbm, out_ref,
    mem, st, wq, wkv, wo, q, kv, ctx, pd, rd, px, rx, part, staged,
    load_sem, stage_sem, send_sem, recv_ici, recv_d2d, st_ici, st_d2d, pd_sem, px_sem,
):
    xs, highs = n_tensor // CORES, n_pipe // LOW
    seqs, enc, depth = mem.shape
    rows = st.shape[1]
    pos = enc // n_pipe
    feat = depth // n_tensor
    inner = wq.shape[1]
    pipe = lax.axis_index("pipe")
    tensor = lax.axis_index("tensor")
    hi, lo = pipe // LOW, pipe % LOW
    x, core = tensor // CORES, tensor % CORES
    other_lo, other_core = 1 - lo, 1 - core

    def turn(a, k, n):
        return lax.rem(a + k, n)

    def device(h, l, xx, c):
        return (h * LOW + l, xx * CORES + c)

    x_peers = [device(hi, lo, turn(x, j, xs), core) for j in range(1, xs)]
    hi_peers = [device(turn(hi, k, highs), lo, x, core) for k in range(1, highs)]
    lo_peer = device(hi, other_lo, x, core)
    sibling = device(hi, lo, x, other_core)

    def block(s, p, xx, c):
        r = pl.multiple_of(p * pos, pos)
        f = pl.multiple_of((xx * CORES + c) * feat, feat)
        return mem.at[s, pl.ds(r, pos), pl.ds(f, feat)]

    def st_block(s, xx, c):
        return st.at[s, :, pl.ds(pl.multiple_of((xx * CORES + c) * feat, feat), feat)]

    sends = []
    counter = [0]

    def new_sems(n=1):
        first = counter[0]
        counter[0] += n
        return first

    def remote(src, dst, sem, recv, dev):
        return pltpu.make_async_remote_copy(
            src_ref=src, dst_ref=dst, send_sem=send_sem.at[sem], recv_sem=recv,
            device_id=dev, device_id_type=MESH,
        )

    def send(src, dst, recv, dev):
        copy = remote(src, dst, new_sems(), recv, dev)
        copy.start()
        sends.append(copy)
        return copy

    st_sends = [[], []]

    def send_states(s, ref, recv, dev):
        st_sends[s].append(send(ref, ref, recv, dev))
        sends.pop()

    def send_block(s, p, xx, dev, recv):
        ref = block(s, p, xx, core)
        send(ref, ref, recv.at[s, p * xs + xx], dev)

    def wait_block(s, p, xx):
        ref = block(s, p, xx, core)
        remote(ref, ref, 0, recv_ici.at[s, p * xs + xx], sibling).wait_recv()

    loads = [
        pltpu.make_async_copy(mem_hbm.at[0], block(0, pipe, x, core), load_sem.at[0]),
        pltpu.make_async_copy(st_hbm.at[0], st_block(0, x, core), load_sem.at[1]),
        pltpu.make_async_copy(mem_hbm.at[1], block(1, pipe, x, core), load_sem.at[2]),
        pltpu.make_async_copy(st_hbm.at[1], st_block(1, x, core), load_sem.at[3]),
    ]
    weights = [
        pltpu.make_async_copy(wq_hbm, wq, load_sem.at[4]),
        pltpu.make_async_copy(wo_hbm, wo, load_sem.at[5]),
    ]
    for copy in loads:
        copy.start()
    barrier = pltpu.get_barrier_semaphore()
    peers = x_peers + hi_peers + [lo_peer, sibling]
    for peer in peers:
        pl.semaphore_signal(barrier, inc=1, device_id=peer, device_id_type=MESH)
    pl.semaphore_wait(barrier, len(peers))

    def first_sends(s):
        loads[2 * s].wait()
        for dev in x_peers:
            send_block(s, pipe, x, dev, recv_ici)
        send_block(s, pipe, x, lo_peer, recv_ici)
        for dev in hi_peers:
            send_block(s, pipe, x, dev, recv_ici)
        send_block(s, pipe, x, sibling, recv_d2d)

    def state_sends(s):
        loads[2 * s + 1].wait()
        ref = st_block(s, x, core)
        for dev in x_peers:
            send_states(s, ref, st_ici.at[s, x], dev)
        send_states(s, ref, st_d2d.at[s, x], sibling)

    def forward_x(s):
        for j in range(1, xs):
            xx = turn(x, j, xs)
            wait_block(s, pipe, xx)
            send_block(s, pipe, xx, lo_peer, recv_ici)
            for dev in hi_peers:
                send_block(s, pipe, xx, dev, recv_ici)
            send_block(s, pipe, xx, sibling, recv_d2d)

    n_high = (highs - 1) * xs

    def high_copies(s, i, base):
        k, j = 1 + i // xs, i % xs
        p, xx = turn(hi, k, highs) * LOW + lo, turn(x, j, xs)
        ref = block(s, p, xx, core)
        slot = p * xs + xx
        arrived = remote(ref, ref, 0, recv_ici.at[s, slot], sibling)
        return (
            arrived,
            remote(ref, ref, base + 2 * i, recv_ici.at[s, slot], lo_peer),
            remote(ref, ref, base + 2 * i + 1, recv_d2d.at[s, slot], sibling),
        )

    def forward_high(s, i, base):
        arrived, over_low, over = high_copies(s, i, base)
        arrived.wait_recv()
        over_low.start()
        over.start()

    high_base = [new_sems(2 * n_high), new_sems(2 * n_high)]

    def forward_low(s):
        for k in range(highs):
            for j in range(xs):
                p, xx = turn(hi, k, highs) * LOW + other_lo, turn(x, j, xs)
                wait_block(s, p, xx)
                send_block(s, p, xx, sibling, recv_d2d)

    def forward_states(s):
        for j in range(1, xs):
            xx = turn(x, j, xs)
            ref = st_block(s, xx, core)
            remote(ref, ref, 0, st_ici.at[s, xx], sibling).wait_recv()
            send_states(s, ref, st_d2d.at[s, xx], sibling)

    def finish_states(s):
        for xx in range(xs):
            ref = st_block(s, xx, other_core)
            remote(ref, ref, 0, st_d2d.at[s, xx], sibling).wait_recv()

    def finish_memory(s):
        for p in range(n_pipe):
            for xx in range(xs):
                ref = block(s, p, xx, other_core)
                remote(ref, ref, 0, recv_d2d.at[s, p * xs + xx], sibling).wait_recv()

    def query(s):
        for copy in st_sends[s]:
            copy.wait_send()
        part[s] = st[s, :, pl.ds(pl.multiple_of(tensor * feat, feat), feat)].astype(F32)

        @pl.loop(0, rows // 16)
        def _(i):
            some = pl.ds(pl.multiple_of(i * 16, 16), 16)
            xf = st[s, some, :].astype(F32)
            mean = jnp.sum(xf * xf, axis=-1, keepdims=True) * (1.0 / depth)
            scale = lax.rsqrt(mean + 1e-06)
            st[s, some, :] = (xf * scale * gain_ref[...]).astype(BF16)

        if s == 0:
            weights[0].wait()

        @pl.loop(0, inner // TILE)
        def _(i):
            cols = pl.ds(pl.multiple_of(i * TILE, TILE), TILE)
            full = jnp.dot(st[s], wq[:, cols], preferred_element_type=F32)
            q[s, :, cols] = full.astype(BF16) * jnp.array(HEAD_DIM ** -0.5, BF16)

    def kv_tile(s, i):
        cols = pl.ds(pl.multiple_of(i * TILE, TILE), TILE)
        full = jnp.dot(mem[s], wkv[:, cols], preferred_element_type=F32)
        kv[:, cols] = full.astype(BF16)

    def attention(s):
        lane = lax.broadcasted_iota(jnp.int32, (1, 2 * HEAD_DIM), 1)
        first = lane < HEAD_DIM

        @pl.loop(0, inner // (2 * HEAD_DIM))
        def _(i):
            cols = pl.ds(pl.multiple_of(i * 2 * HEAD_DIM, 2 * HEAD_DIM), 2 * HEAD_DIM)
            vcols = pl.ds(pl.multiple_of(inner + i * 2 * HEAD_DIM, 2 * HEAD_DIM), 2 * HEAD_DIM)
            qp, kp, vp = q[s, :, cols], kv[:, cols], kv[:, vcols]
            outs = []
            for mine in (first, jnp.logical_not(first)):
                qh = jnp.where(mine, qp, jnp.zeros_like(qp))
                vh = jnp.where(mine, vp, jnp.ones_like(vp))
                scores = lax.dot_general(
                    qh, kp, (((1,), (1,)), ((), ())), preferred_element_type=F32
                )
                top = jnp.max(scores, axis=-1, keepdims=True)
                probs = jnp.exp(scores - top).astype(BF16)
                outs.append(jnp.dot(probs, vh, preferred_element_type=F32))
            total = jnp.where(first, outs[0], outs[1])
            sums = pltpu.roll(jnp.where(first, outs[1], outs[0]), HEAD_DIM, 1)
            ctx[:, cols] = (total / sums).astype(BF16)

    width = min(TILE, feat)

    def product(t, i):
        cols = pl.ds(pl.multiple_of(t * feat + i * width, width), width)
        return jnp.dot(ctx[...], wo[:, cols], preferred_element_type=F32)

    def tile(i):
        return pl.ds(pl.multiple_of(i * width, width), width)

    def output(s):
        if s == 0:
            weights[1].wait()
        steps = feat // width
        order = [turn(x, j, xs) for j in range(1, xs)] + [x]
        for j, xx in enumerate(order):
            @pl.loop(0, steps)
            def _(i):
                pd[s, j, :, tile(i)] = product(xx * CORES + other_core, i).astype(BF16)

            send(pd.at[s, j], rd.at[s, j], pd_sem.at[s, j], sibling)
            if j < xs - 1:
                @pl.loop(0, steps)
                def _(i):
                    px[s, j, :, tile(i)] = product(xx * CORES + core, i).astype(BF16)

                remote(pd.at[s, j], rd.at[s, j], 0, pd_sem.at[s, j], sibling).wait_recv()
                px[s, j] = (px[s, j].astype(F32) + rd[s, j].astype(F32)).astype(BF16)
                send(px.at[s, j], rx.at[s, j], px_sem.at[s, j], x_peers[j])

    def result(s):
        j = xs - 1
        remote(pd.at[s, j], rd.at[s, j], 0, pd_sem.at[s, j], sibling).wait_recv()

        @pl.loop(0, feat // width)
        def _(i):
            c = tile(i)
            part[s, :, c] += product(tensor, i) + rd[s, j, :, c].astype(F32)

    def finish(s):
        for j in range(xs - 1):
            remote(px.at[s, j], rx.at[s, j], 0, px_sem.at[s, j], sibling).wait_recv()

        @pl.loop(0, feat // width)
        def _(i):
            c = tile(i)
            total = part[s, :, c]
            for j in range(xs - 1):
                total += rx[s, j, :, c].astype(F32)
            out_ref[s, :, c] = total.astype(BF16)

    groups = 2 * inner // LANES
    size = CHUNK * groups
    chunks = depth // CHUNK

    def stage(i, slot):
        src = wkv_hbm.at[pl.ds(pl.multiple_of(i * size, size), size), :]
        return pltpu.make_async_copy(src, staged.at[slot], stage_sem.at[slot])

    def spread(begin, end):
        span = SUB * groups
        a = lax.broadcasted_iota(jnp.int32, (span, span), 0)
        b = lax.broadcasted_iota(jnp.int32, (span, span), 1)
        swap = (b == lax.rem(a, SUB) * groups + a // SUB).astype(F32).astype(BF16)

        @pl.loop(begin, end)
        def _(i):
            slot = lax.rem(i, 2)
            stage(i, slot).wait()

            @pl.loop(0, CHUNK // (2 * SUB))
            def _(m):
                r = pl.multiple_of(m * 2 * span, 2 * span)
                both = jnp.concatenate(
                    [staged[slot, pl.ds(r, span), :], staged[slot, pl.ds(r + span, span), :]], axis=1
                )
                moved = jnp.dot(swap, both, preferred_element_type=F32).astype(BF16)
                d = pl.multiple_of(i * CHUNK + m * 2 * SUB, 2 * SUB)
                for g in range(groups):
                    col = (g % 2) * inner + (g // 2) * LANES
                    piece = moved[g * SUB:(g + 1) * SUB]
                    wkv[pl.ds(d, SUB), col:col + LANES] = piece[:, :LANES]
                    wkv[pl.ds(d + SUB, SUB), col:col + LANES] = piece[:, LANES:]

            @pl.when(i + 2 < chunks)
            def _():
                stage(i + 2, slot).start()

    for i in range(2):
        stage(i, i).start()
    for s in range(seqs):
        first_sends(s)
        state_sends(s)
        if s == 0:
            for copy in weights:
                copy.start()
    spread(0, chunks // 4)
    forward_x(0)
    spread(chunks // 4, chunks)
    half = n_high // 2
    for i in range(half):
        forward_high(0, i, high_base[0])
    forward_x(1)
    for i in range(half, n_high):
        forward_high(0, i, high_base[0])
    forward_states(0)
    finish_states(0)
    query(0)
    forward_low(0)
    forward_states(1)
    finish_states(1)
    query(1)
    finish_memory(0)
    tiles = 2 * inner // TILE

    @pl.loop(0, tiles)
    def _(i):
        @pl.when(i < n_high)
        def _():
            forward_high(1, i, high_base[1])

        kv_tile(0, i)

    for i in range(tiles, n_high):
        forward_high(1, i, high_base[1])
    attention(0)
    output(0)
    forward_low(1)
    result(0)
    finish_memory(1)

    @pl.loop(0, tiles)
    def _(i):
        kv_tile(1, i)

    attention(1)
    output(1)
    result(1)
    finish(0)
    finish(1)
    for copy in sends:
        copy.wait_send()
    for s in range(seqs):
        for i in range(n_high):
            arrived, over_low, over = high_copies(s, i, high_base[s])
            over_low.wait_send()
            over.wait_send()


def fused(n_pipe, n_tensor, memory, states, norm_gain, w_query, w_keyvalue, w_output):
    seqs, pos, feat = memory.shape
    rows = states.shape[2]
    depth, inner = feat * n_tensor, w_query.shape[2]
    enc = pos * n_pipe
    xs, highs = n_tensor // CORES, n_pipe // LOW
    groups = 2 * inner // LANES
    weight_kv = w_keyvalue[0].reshape(depth, 2, inner // LANES, LANES)
    weight_kv = weight_kv.transpose(0, 2, 1, 3).reshape(depth * groups, LANES)
    blocks = n_pipe * xs
    per_seq = ((xs - 1) + (highs - 1) + 2 + (xs - 1) * (highs + 1) + 2 * (highs - 1) * xs
               + highs * xs + 2 * xs + 2 * xs)
    any_space = pl.BlockSpec(memory_space=pl.ANY)
    in_vmem = pl.BlockSpec(memory_space=pltpu.VMEM)
    dma = pltpu.SemaphoreType.DMA
    out = pl.pallas_call(
        functools.partial(kernel, n_pipe, n_tensor),
        out_shape=jax.ShapeDtypeStruct((seqs, rows, feat), BF16),
        in_specs=[any_space, any_space, in_vmem, any_space, any_space, any_space],
        out_specs=in_vmem,
        scratch_shapes=[
            pltpu.VMEM((seqs, enc, depth), BF16),
            pltpu.VMEM((seqs, rows, depth), BF16),
            pltpu.VMEM((depth, inner), BF16),
            pltpu.VMEM((depth, 2 * inner), BF16),
            pltpu.VMEM((inner, depth), BF16),
            pltpu.VMEM((seqs, rows, inner), BF16),
            pltpu.VMEM((enc, 2 * inner), BF16),
            pltpu.VMEM((rows, inner), BF16),
            pltpu.VMEM((seqs, xs, rows, feat), BF16),
            pltpu.VMEM((seqs, xs, rows, feat), BF16),
            pltpu.VMEM((seqs, xs - 1, rows, feat), BF16),
            pltpu.VMEM((seqs, xs - 1, rows, feat), BF16),
            pltpu.VMEM((seqs, rows, feat), F32),
            pltpu.VMEM((2, CHUNK * groups, LANES), BF16),
            dma((6,)),
            dma((2,)),
            dma((seqs * per_seq,)),
            dma((seqs, blocks)),
            dma((seqs, blocks)),
            dma((seqs, xs)),
            dma((seqs, xs)),
            dma((seqs, xs)),
            dma((seqs, xs - 1)),
        ],
        compiler_params=pltpu.CompilerParams(
            collective_id=0, has_side_effects=True, vmem_limit_bytes=66_000_000
        ),
    )(memory, states[0], norm_gain, w_query[0], weight_kv, w_output[0])
    return out[None]


def per_device(memory, states, norm_gain, w_query, w_keyvalue, w_output):
    whole_states = lax.all_gather(states[0], "tensor", axis=2, tiled=True)
    xf = whole_states.astype(jnp.float32)
    scale = lax.rsqrt(jnp.mean(xf * xf, axis=-1, keepdims=True) + 1e-06)
    normed = (xf * scale * norm_gain[0]).astype(jnp.bfloat16)
    weight_q = w_query[0]
    local_inner = weight_q.shape[1]
    weight_kv = w_keyvalue[0].reshape(w_keyvalue.shape[1], 2 * local_inner)
    weight_o = w_output[0]
    seqs = normed.shape[0]
    dec_rows = normed.shape[1]
    local_heads = local_inner // HEAD_DIM
    query = jnp.einsum("btd,de->bte", normed, weight_q, preferred_element_type=jnp.float32).astype(
        jnp.bfloat16
    )
    gathered = lax.all_gather(memory, "pipe", axis=1, tiled=True)
    gathered = lax.all_gather(gathered, "tensor", axis=2, tiled=True)
    keyvalue = jnp.einsum(
        "bpd,de->bpe", gathered, weight_kv, preferred_element_type=jnp.float32
    ).astype(jnp.bfloat16)
    enc_rows = keyvalue.shape[1]
    keys = keyvalue[:, :, :local_inner].reshape(seqs, enc_rows, local_heads, HEAD_DIM)
    values = keyvalue[:, :, local_inner:].reshape(seqs, enc_rows, local_heads, HEAD_DIM)
    heads_q = query.reshape(seqs, dec_rows, local_heads, HEAD_DIM)
    scores = jnp.einsum(
        "bqhd,bkhd->bhqk", heads_q, keys, preferred_element_type=jnp.float32
    ) / jnp.sqrt(jnp.float32(HEAD_DIM))
    probs = jax.nn.softmax(scores, axis=-1).astype(jnp.bfloat16)
    context = jnp.einsum(
        "bhqk,bkhd->bqhd", probs, values, preferred_element_type=jnp.float32
    ).astype(jnp.bfloat16)
    context = context.reshape(seqs, dec_rows, local_inner)
    partial_terms = jnp.einsum("bte,ed->btd", context, weight_o, preferred_element_type=jnp.float32)
    branch = lax.psum_scatter(partial_terms, "tensor", scatter_dimension=2, tiled=True)
    result = (states[0].astype(jnp.float32) + branch).astype(jnp.bfloat16)
    return result[None]


def solution(mesh):
    in_specs = (
        P(None, "pipe", "tensor"),
        P("pipe", None, None, "tensor"),
        P("pipe", None),
        P("pipe", None, "tensor"),
        P("pipe", None, None, "tensor"),
        P("pipe", "tensor", None),
    )
    out_specs = P("pipe", None, None, "tensor")
    n_pipe, n_tensor = mesh.shape["pipe"], mesh.shape["tensor"]
    even = n_pipe % LOW == 0 and n_tensor % CORES == 0 and n_pipe > LOW and n_tensor > CORES
    body = per_device
    if even and copies_per_sequence(n_pipe, n_tensor) <= MAX_COPIES:
        body = functools.partial(fused, n_pipe, n_tensor)
    return jax.shard_map(
        body, mesh=mesh, in_specs=in_specs, out_specs=out_specs, check_vma=False
    )
```

profile of v0, /device:TPU:8, one launch (start us, length us, event | category | flops | bytes accessed | tf_op | source)
XLA Modules:
  0.0 133.0 jit_solution(17757589553315950088)
XLA Ops:
  0.0 130.7 %shard_map.64 = bf16[2,256,1024]{2,1,0:T(8,128)(2,1)} custom-call(bf16[2,64,1024]{2,1,0:T(8,128)(2,1)} %mem_hbm.1, bf16[2,256,1024]{2,1,0:T(8,128)(2,1)} %bitcast.13, f32[1,4096]{1,0:T(1,128)} %gain_ref.1, bf16[4096,1024]{1,0:T(8,128)(2,1)} %bitcast.10, bf16[65536,128]{1,0:T(8,128)(2,1)} %bitcast.9, bf16[1024,4096]{1,0:T(8,128)(2,1)} %bitcast.11), custom_call_target="tpu_custom_call" | custom-call | tf_op jit(solution)/shard_map/pallas_call | solution.py:402
  130.7 2.3 %copy.9 = bf16[1,2,256,1024]{3,2,1,0:T(8,128)(2,1)} copy(bf16[1,2,256,1024]{3,2,1,0:T(8,128)(2,1)} %bitcast.12) | data formatting | bytes 2097152
where the time goes:
time: 133 us
  Pallas kernels  131 us (98%)
  local copies, waits for them, and re-layouts  2.26 us (2%)
    pallas_call x1, Pallas kernels, fused(): pl.pallas_call(functools.partial(kernel, n_pipe, n_tensor), out_shape=jax...  131 us

commit v1 on v0

v1 whole, which is shorter than its diff:
```python
import functools

import jax
import jax.numpy as jnp
from jax import lax
from jax.experimental import pallas as pl
from jax.experimental.pallas import tpu as pltpu
from jax.sharding import PartitionSpec as P

HEAD_DIM = 64
CORES = 2
LOW = 2
TILE = 256
WIDE = 512
MAX_COPIES = 100
LANES = 128
SUB = 16
CHUNK = 256
SLOTS = 3
MESH = pl.DeviceIdType.MESH
F32 = jnp.float32
BF16 = jnp.bfloat16


def copies_per_sequence(n_pipe, n_tensor):
    xs, highs = n_tensor // CORES, n_pipe // LOW
    return 4 * n_pipe * xs + (xs - 1) * highs


def kernel(
    n_pipe, n_tensor,
    mem_hbm, st_hbm, gain_ref, wq_hbm, wkv_hbm, wo_hbm, out_hbm,
    mem, st, wq, wkv, wo, q, kv, ctx, pd, rd, px, rx, part, staged, squares, done,
    load_sem, stage_sem, send_sem, recv_ici, recv_d2d, st_ici, st_d2d, pd_sem, px_sem, out_sem,
):
    xs, highs = n_tensor // CORES, n_pipe // LOW
    seqs, enc, depth = mem.shape
    rows = st.shape[1]
    pos = enc // n_pipe
    feat = depth // n_tensor
    inner = wq.shape[1]
    pipe = lax.axis_index("pipe")
    tensor = lax.axis_index("tensor")
    hi, lo = pipe // LOW, pipe % LOW
    x, core = tensor // CORES, tensor % CORES
    other_lo, other_core = 1 - lo, 1 - core
    scope = jax.named_scope

    def turn(a, k, n):
        return lax.rem(a + k, n)

    def device(h, l, xx, c):
        return (h * LOW + l, xx * CORES + c)

    x_peers = [device(hi, lo, turn(x, j, xs), core) for j in range(1, xs)]
    hi_peers = [device(turn(hi, k, highs), lo, x, core) for k in range(1, highs)]
    lo_peer = device(hi, other_lo, x, core)
    sibling = device(hi, lo, x, other_core)

    def block(s, h, far, xx, c):
        r = pl.multiple_of((far * highs + h) * pos, pos)
        f = pl.multiple_of((xx * CORES + c) * feat, feat)
        return mem.at[s, pl.ds(r, pos), pl.ds(f, feat)]

    def slot(h, l, xx):
        return (h * LOW + l) * xs + xx

    def st_block(s, xx, c):
        return st.at[s, :, pl.ds(pl.multiple_of((xx * CORES + c) * feat, feat), feat)]

    counter = [0]
    waits = []

    def remote(src, dst, sem, recv, dev):
        return pltpu.make_async_remote_copy(
            src_ref=src, dst_ref=dst, send_sem=send_sem.at[sem], recv_sem=recv,
            device_id=dev, device_id_type=MESH,
        )

    def send(src, dst, recv, dev, like, keep=True):
        sem = counter[0]
        counter[0] += 1
        remote(src, dst, sem, recv, dev).start()
        if keep:
            waits.append((like, sem))
        return sem

    def sent(like, sem):
        remote(like, like, sem, recv_ici.at[0, 0], sibling).wait_send()

    def like_block():
        return block(0, 0, 0, 0, 0)

    def send_own(s, h, xx, dev, recv):
        ref = block(s, h, 0, xx, core)
        send(ref, ref, recv.at[s, slot(h, lo, xx)], dev, like_block)

    def send_low(s, h, xx):
        send(block(s, h, 0, xx, core), block(s, h, 1, xx, core),
             recv_ici.at[s, slot(h, lo, xx)], lo_peer, like_block)

    def send_far(s, h, xx):
        ref = block(s, h, 1, xx, core)
        send(ref, ref, recv_d2d.at[s, slot(h, other_lo, xx)], sibling, like_block)

    def arrived(s, h, l, xx, recv):
        ref = like_block()
        remote(ref, ref, 0, recv.at[s, slot(h, l, xx)], sibling).wait_recv()

    st_sends = [[], []]

    def first_send(s):
        def low():
            send_low(s, hi, x)

        def across():
            for dev in x_peers:
                send_own(s, hi, x, dev, recv_ici)

        def high():
            for dev in hi_peers:
                send_own(s, hi, x, dev, recv_ici)

        def over():
            send_own(s, hi, x, sibling, recv_d2d)

        return low, across, high, over

    def state_sends(s):
        ref = st_block(s, x, core)
        for dev in x_peers:
            st_sends[s].append(send(ref, ref, st_ici.at[s, x], dev, None, False))
        st_sends[s].append(send(ref, ref, st_d2d.at[s, x], sibling, None, False))

    def forward_x(s):
        for j in range(1, xs):
            xx = turn(x, j, xs)
            arrived(s, hi, lo, xx, recv_ici)
            send_low(s, hi, xx)
            for dev in hi_peers:
                send_own(s, hi, xx, dev, recv_ici)
            send_own(s, hi, xx, sibling, recv_d2d)

    high_order = [(k, j) for j in range(xs) for k in range(highs - 1, 0, -1)]
    low_order = [(0, j) for j in range(xs)] + high_order

    def forward_high(s, i):
        k, j = high_order[i]
        h, xx = turn(hi, k, highs), turn(x, j, xs)
        arrived(s, h, lo, xx, recv_ici)
        send_low(s, h, xx)
        send_own(s, h, xx, sibling, recv_d2d)

    def forward_low(s, i):
        k, j = low_order[i]
        h, xx = turn(hi, k, highs), turn(x, j, xs)
        arrived(s, h, other_lo, xx, recv_ici)
        send_far(s, h, xx)

    def forward_states(s):
        for j in range(1, xs):
            xx = turn(x, j, xs)
            ref = st_block(s, xx, core)
            remote(ref, ref, 0, st_ici.at[s, xx], sibling).wait_recv()
            st_sends[s].append(send(ref, ref, st_d2d.at[s, xx], sibling, None, False))

    def finish_states(s):
        for xx in range(xs):
            ref = st_block(s, xx, other_core)
            remote(ref, ref, 0, st_d2d.at[s, xx], sibling).wait_recv()
        for sem in st_sends[s]:
            sent(st_block(s, x, core), sem)

    def finish_memory(s, far):
        for h in range(highs):
            for xx in range(xs):
                arrived(s, h, other_lo if far else lo, xx, recv_d2d)

    def steps(n, body, plan=()):
        plan = dict(plan)
        assert all(t < n for t in plan)

        @pl.loop(0, n)
        def _(i):
            for t, events in plan.items():
                @pl.when(i == t)
                def _(events=events):
                    for fn, *args in events:
                        fn(*args)

            body(i)

    def do(*events):
        for fn, *args in events:
            fn(*args)

    def normalize(s):
        part[s] = st[s, :, pl.ds(pl.multiple_of(tensor * feat, feat), feat)].astype(F32)

        @pl.loop(0, rows // SUB)
        def _(i):
            some = pl.ds(pl.multiple_of(i * SUB, SUB), SUB)
            total = jnp.zeros((SUB, LANES), F32)
            for g in range(depth // LANES):
                cols = slice(g * LANES, (g + 1) * LANES)
                xf = st[s, some, cols].astype(F32)
                total += xf * xf
                st[s, some, cols] = (xf * gain_ref[:, cols]).astype(BF16)
            squares[some, :] = total

        mean = jnp.sum(squares[...], axis=-1, keepdims=True) * (1.0 / depth)
        scale = lax.rsqrt(mean + 1e-06) * (HEAD_DIM ** -0.5)
        squares[...] = jnp.broadcast_to(scale, squares.shape)

    def query(s, plan):
        def body(i):
            cols = pl.ds(pl.multiple_of(i * TILE, TILE), TILE)
            full = jnp.dot(st[s], wq[:, cols], preferred_element_type=F32)
            scale = squares[...]
            q[s, :, cols] = (full * jnp.concatenate([scale] * (TILE // LANES), axis=1)).astype(BF16)

        steps(inner // TILE, body, plan)

    half = highs * pos

    def keyvalue(s, far, plan):
        def body(i):
            cols = pl.ds(pl.multiple_of(i * WIDE, WIDE), WIDE)
            full = jnp.dot(mem[s, far * half:(far + 1) * half], wkv[:, cols], preferred_element_type=F32)
            kv[far * half:(far + 1) * half, cols] = full.astype(BF16)

        steps(2 * inner // WIDE, body, plan)

    PAIRS = 2

    def attention(s, plan):
        lane = lax.broadcasted_iota(jnp.int32, (1, 2 * HEAD_DIM), 1)
        first = lane < HEAD_DIM

        def body(step):
            for u in range(PAIRS):
                i = step * PAIRS + u
                cols = pl.ds(pl.multiple_of(i * 2 * HEAD_DIM, 2 * HEAD_DIM), 2 * HEAD_DIM)
                vcols = pl.ds(pl.multiple_of(inner + i * 2 * HEAD_DIM, 2 * HEAD_DIM), 2 * HEAD_DIM)
                qp, kp, vp = q[s, :, cols], kv[:, cols], kv[:, vcols]
                outs = []
                for mine in (first, jnp.logical_not(first)):
                    qh = jnp.where(mine, qp, jnp.zeros_like(qp))
                    vh = jnp.where(mine, vp, jnp.ones_like(vp))
                    scores = lax.dot_general(
                        qh, kp, (((1,), (1,)), ((), ())), preferred_element_type=F32
                    )
                    top = jnp.max(scores, axis=-1, keepdims=True)
                    probs = jnp.exp(scores - top).astype(BF16)
                    outs.append(jnp.dot(probs, vh, preferred_element_type=F32))
                total = jnp.where(first, outs[0], outs[1])
                sums = pltpu.roll(jnp.where(first, outs[1], outs[0]), HEAD_DIM, 1)
                ctx[:, cols] = (total / sums).astype(BF16)

        steps(inner // (2 * HEAD_DIM * PAIRS), body, plan)

    width = min(WIDE, feat)
    tiles = feat // width

    def product(t, i):
        cols = pl.ds(pl.multiple_of(t * feat + i * width, width), width)
        return jnp.dot(ctx[...], wo[:, cols], preferred_element_type=F32)

    def output(s):
        order = [turn(x, j, xs) for j in range(1, xs)] + [x]

        def over(j, i):
            c = slice(i * width, (i + 1) * width)
            pd[s, j, :, c] = product(order[j] * CORES + other_core, i).astype(BF16)
            send(pd.at[s, j, :, c], rd.at[s, j, :, c], pd_sem.at[s, j, i], sibling,
                 lambda: pd.at[0, 0, :, :width])

        def back(j, i):
            c = slice(i * width, (i + 1) * width)
            remote(pd.at[s, j, :, c], rd.at[s, j, :, c], 0, pd_sem.at[s, j, i], sibling).wait_recv()

        for j in range(xs - 1):
            for i in range(tiles):
                over(j, i)
            for i in range(tiles):
                c = slice(i * width, (i + 1) * width)
                mine = product(order[j] * CORES + core, i)
                back(j, i)
                px[s, j, :, c] = (mine + rd[s, j, :, c].astype(F32)).astype(BF16)
                send(px.at[s, j, :, c], rx.at[s, j, :, c], px_sem.at[s, j, i], x_peers[j],
                     lambda: pd.at[0, 0, :, :width])
        j = xs - 1
        for i in range(tiles):
            over(j, i)
        for i in range(tiles):
            c = slice(i * width, (i + 1) * width)
            part[s, :, c] += product(tensor, i)
        for i in range(tiles):
            c = slice(i * width, (i + 1) * width)
            back(j, i)
            part[s, :, c] += rd[s, j, :, c].astype(F32)

    def out_copy(s, i):
        c = slice(i * width, (i + 1) * width)
        return pltpu.make_async_copy(done.at[s, :, c], out_hbm.at[s, :, c], out_sem.at[s, i])

    def finish(s):
        for i in range(tiles):
            c = slice(i * width, (i + 1) * width)
            total = part[s, :, c]
            for j in range(xs - 1):
                remote(px.at[s, j, :, c], rx.at[s, j, :, c], 0, px_sem.at[s, j, i], sibling).wait_recv()
                total += rx[s, j, :, c].astype(F32)
            done[s, :, c] = total.astype(BF16)
            out_copy(s, i).start()

    groups = 2 * inner // LANES
    size = CHUNK * groups
    chunks = depth // CHUNK
    slots = staged.shape[0]

    def stage(i, slot):
        src = wkv_hbm.at[pl.ds(pl.multiple_of(i * size, size), size), :]
        return pltpu.make_async_copy(src, staged.at[slot], stage_sem.at[slot])

    def spread(plan):
        span = SUB * groups
        a = lax.broadcasted_iota(jnp.int32, (span, span), 0)
        b = lax.broadcasted_iota(jnp.int32, (span, span), 1)
        swap = (b == lax.rem(a, SUB) * groups + a // SUB).astype(F32).astype(BF16)

        def body(i):
            slot = lax.rem(i, slots)
            stage(i, slot).wait()
            for m in range(CHUNK // (2 * SUB)):
                r = m * 2 * span
                both = jnp.concatenate(
                    [staged[slot, r:r + span, :], staged[slot, r + span:r + 2 * span, :]], axis=1
                )
                moved = jnp.dot(swap, both, preferred_element_type=F32).astype(BF16)
                d = pl.multiple_of(i * CHUNK + m * 2 * SUB, 2 * SUB)
                for g in range(groups):
                    col = (g % 2) * inner + (g // 2) * LANES
                    piece = moved[g * SUB:(g + 1) * SUB]
                    wkv[pl.ds(d, SUB), col:col + LANES] = piece[:, :LANES]
                    wkv[pl.ds(d + SUB, SUB), col:col + LANES] = piece[:, LANES:]

            @pl.when(i + slots < chunks)
            def _():
                stage(i + slots, slot).start()

        steps(chunks, body, plan)

    loads = [
        pltpu.make_async_copy(mem_hbm.at[0], block(0, hi, 0, x, core), load_sem.at[0]),
        pltpu.make_async_copy(st_hbm.at[0], st_block(0, x, core), load_sem.at[1]),
        pltpu.make_async_copy(mem_hbm.at[1], block(1, hi, 0, x, core), load_sem.at[2]),
        pltpu.make_async_copy(st_hbm.at[1], st_block(1, x, core), load_sem.at[3]),
    ]
    weights = [
        pltpu.make_async_copy(wq_hbm, wq, load_sem.at[4]),
        pltpu.make_async_copy(wo_hbm, wo, load_sem.at[5]),
    ]
    for copy in loads:
        copy.start()
    barrier = pltpu.get_barrier_semaphore()
    peers = x_peers + hi_peers + [lo_peer, sibling]
    for peer in peers:
        pl.semaphore_signal(barrier, inc=1, device_id=peer, device_id_type=MESH)
    for i in range(slots):
        stage(i, i).start()
    for copy in weights:
        copy.start()
    with scope("barrier"):
        pl.semaphore_wait(barrier, len(peers))
    with scope("load0"):
        loads[0].wait()
    low, across, high, over = first_send(0)
    across(), low(), high(), over()
    with scope("load1"):
        loads[1].wait()
    state_sends(0)
    loads[2].wait()
    loads[3].wait()
    low1, across1, high1, over1 = first_send(1)

    def second_start():
        high1()
        across1()
        over1()
        state_sends(1)

    def fx(s): forward_x(s)
    def fh(s, i): forward_high(s, i)
    def fl(s, i): forward_low(s, i)

    with scope("spread"):
        spread({
            8: [(fx, 0), (second_start,)],
            9: [(fl, 0, 0)],
            10: [(fh, 0, 0)],
            12: [(fh, 0, 1)],
            14: [(fl, 0, 1)],
        })
    with scope("fh02"):
        fh(0, 2)
    with scope("fl02"):
        fl(0, 2)
    with scope("fh03"):
        fh(0, 3)
    low1()
    with scope("fl03"):
        fl(0, 3)
    with scope("fst0"):
        forward_states(0)
    with scope("finst0"):
        finish_states(0)
    with scope("norm0"):
        normalize(0)
    with scope("wq"):
        weights[0].wait()
    with scope("query0"):
        query(0, {0: [(fh, 0, 4)], 1: [(fl, 0, 4)], 2: [(fh, 0, 5)], 3: [(fl, 0, 5)]})
    with scope("finmem00"):
        finish_memory(0, 0)
    with scope("kv00"):
        keyvalue(0, 0, {0: [(fx, 1)], 1: [(fl, 0, 6)], 2: [(fh, 1, 0)], 3: [(fl, 0, 7)]})
    with scope("finmem01"):
        finish_memory(0, 1)
    with scope("kv01"):
        keyvalue(0, 1, {0: [(fh, 1, 1)], 1: [(fl, 1, 0)], 2: [(fh, 1, 2)], 3: [(fl, 1, 1)]})
    with scope("att0"):
        attention(0, {0: [(fh, 1, 3)], 1: [(fl, 1, 2)], 2: [(fh, 1, 4), (forward_states, 1)], 3: [(fl, 1, 3)]})
    with scope("fh15"):
        fh(1, 5)
    with scope("finst1"):
        finish_states(1)
    with scope("norm1"):
        normalize(1)
    with scope("query1"):
        query(1, {1: [(fl, 1, 4)], 3: [(fl, 1, 5)]})
    weights[1].wait()
    with scope("output0"):
        output(0)
    with scope("finmem10"):
        finish_memory(1, 0)
    with scope("kv10"):
        keyvalue(1, 0, {1: [(fl, 1, 6)], 3: [(fl, 1, 7)]})
    with scope("finmem11"):
        finish_memory(1, 1)
    with scope("kv11"):
        keyvalue(1, 1, {})
    with scope("finish0"):
        finish(0)
    with scope("att1"):
        attention(1, {})
    with scope("output1"):
        output(1)
    with scope("finish1"):
        finish(1)
    with scope("end"):
        for like, sem in waits:
            sent(like(), sem)
        for s in range(seqs):
            for i in range(tiles):
                out_copy(s, i).wait()


def fused(n_pipe, n_tensor, memory, states, norm_gain, w_query, w_keyvalue, w_output):
    seqs, pos, feat = memory.shape
    rows = states.shape[2]
    depth, inner = feat * n_tensor, w_query.shape[2]
    enc = pos * n_pipe
    xs, highs = n_tensor // CORES, n_pipe // LOW
    groups = 2 * inner // LANES
    weight_kv = w_keyvalue[0].reshape(depth, 2, inner // LANES, LANES)
    weight_kv = weight_kv.transpose(0, 2, 1, 3).reshape(depth * groups, LANES)
    blocks = n_pipe * xs
    tiles = feat // min(WIDE, feat)
    per_seq = ((xs - 1) + (highs - 1) + 2 + (xs - 1) * (highs + 1) + 2 * (highs - 1) * xs
               + highs * xs + 2 * xs + 2 * xs * tiles)
    any_space = pl.BlockSpec(memory_space=pl.ANY)
    in_vmem = pl.BlockSpec(memory_space=pltpu.VMEM)
    dma = pltpu.SemaphoreType.DMA
    out = pl.pallas_call(
        functools.partial(kernel, n_pipe, n_tensor),
        out_shape=jax.ShapeDtypeStruct((seqs, rows, feat), BF16),
        in_specs=[any_space, any_space, in_vmem, any_space, any_space, any_space],
        out_specs=any_space,
        scratch_shapes=[
            pltpu.VMEM((seqs, enc, depth), BF16),
            pltpu.VMEM((seqs, rows, depth), BF16),
            pltpu.VMEM((depth, inner), BF16),
            pltpu.VMEM((depth, 2 * inner), BF16),
            pltpu.VMEM((inner, depth), BF16),
            pltpu.VMEM((seqs, rows, inner), BF16),
            pltpu.VMEM((enc, 2 * inner), BF16),
            pltpu.VMEM((rows, inner), BF16),
            pltpu.VMEM((seqs, xs, rows, feat), BF16),
            pltpu.VMEM((seqs, xs, rows, feat), BF16),
            pltpu.VMEM((seqs, xs - 1, rows, feat), BF16),
            pltpu.VMEM((seqs, xs - 1, rows, feat), BF16),
            pltpu.VMEM((seqs, rows, feat), F32),
            pltpu.VMEM((SLOTS, CHUNK * groups, LANES), BF16),
            pltpu.VMEM((rows, LANES), F32),
            pltpu.VMEM((seqs, rows, feat), BF16),
            dma((6,)),
            dma((SLOTS,)),
            dma((seqs * per_seq,)),
            dma((seqs, blocks)),
            dma((seqs, blocks)),
            dma((seqs, xs)),
            dma((seqs, xs)),
            dma((seqs, xs, tiles)),
            dma((seqs, xs - 1, tiles)),
            dma((seqs, tiles)),
        ],
        compiler_params=pltpu.CompilerParams(
            collective_id=0, has_side_effects=True, vmem_limit_bytes=66_000_000
        ),
    )(memory, states[0], norm_gain, w_query[0], weight_kv, w_output[0])
    return out[None]


def per_device(memory, states, norm_gain, w_query, w_keyvalue, w_output):
    whole_states = lax.all_gather(states[0], "tensor", axis=2, tiled=True)
    xf = whole_states.astype(jnp.float32)
    scale = lax.rsqrt(jnp.mean(xf * xf, axis=-1, keepdims=True) + 1e-06)
    normed = (xf * scale * norm_gain[0]).astype(jnp.bfloat16)
    weight_q = w_query[0]
    local_inner = weight_q.shape[1]
    weight_kv = w_keyvalue[0].reshape(w_keyvalue.shape[1], 2 * local_inner)
    weight_o = w_output[0]
    seqs = normed.shape[0]
    dec_rows = normed.shape[1]
    local_heads = local_inner // HEAD_DIM
    query = jnp.einsum("btd,de->bte", normed, weight_q, preferred_element_type=jnp.float32).astype(
        jnp.bfloat16
    )
    gathered = lax.all_gather(memory, "pipe", axis=1, tiled=True)
    gathered = lax.all_gather(gathered, "tensor", axis=2, tiled=True)
    keyvalue = jnp.einsum(
        "bpd,de->bpe", gathered, weight_kv, preferred_element_type=jnp.float32
    ).astype(jnp.bfloat16)
    enc_rows = keyvalue.shape[1]
    keys = keyvalue[:, :, :local_inner].reshape(seqs, enc_rows, local_heads, HEAD_DIM)
    values = keyvalue[:, :, local_inner:].reshape(seqs, enc_rows, local_heads, HEAD_DIM)
    heads_q = query.reshape(seqs, dec_rows, local_heads, HEAD_DIM)
    scores = jnp.einsum(
        "bqhd,bkhd->bhqk", heads_q, keys, preferred_element_type=jnp.float32
    ) / jnp.sqrt(jnp.float32(HEAD_DIM))
    probs = jax.nn.softmax(scores, axis=-1).astype(jnp.bfloat16)
    context = jnp.einsum(
        "bhqk,bkhd->bqhd", probs, values, preferred_element_type=jnp.float32
    ).astype(jnp.bfloat16)
    context = context.reshape(seqs, dec_rows, local_inner)
    partial_terms = jnp.einsum("bte,ed->btd", context, weight_o, preferred_element_type=jnp.float32)
    branch = lax.psum_scatter(partial_terms, "tensor", scatter_dimension=2, tiled=True)
    result = (states[0].astype(jnp.float32) + branch).astype(jnp.bfloat16)
    return result[None]


def solution(mesh):
    in_specs = (
        P(None, "pipe", "tensor"),
        P("pipe", None, None, "tensor"),
        P("pipe", None),
        P("pipe", None, "tensor"),
        P("pipe", None, None, "tensor"),
        P("pipe", "tensor", None),
    )
    out_specs = P("pipe", None, None, "tensor")
    n_pipe, n_tensor = mesh.shape["pipe"], mesh.shape["tensor"]
    even = n_pipe % LOW == 0 and n_tensor % CORES == 0 and n_pipe > LOW and n_tensor > CORES
    body = per_device
    if even and copies_per_sequence(n_pipe, n_tensor) <= MAX_COPIES:
        body = functools.partial(fused, n_pipe, n_tensor)
    return jax.shard_map(
        body, mesh=mesh, in_specs=in_specs, out_specs=out_specs, check_vma=False
    )
```

time: 133 us -> 102 us (0.77)
  the two profiles are of different devices: /device:TPU:8 before, /device:TPU:29 now
where the time goes in v1:
time: 102 us; the launch traced here: 101 us
  Pallas kernels  99.2 us (97%)
  local copies, waits for them, and re-layouts  2.26 us (2%)
    pallas_call x1, Pallas kernels, fused(): pl.pallas_call(functools.partial(kernel, n_pipe, n_tensor), out_shape=jax...  99.2 us
    unnamed x1, local copies, waits for them, and re-layouts  2.26 us

profile of v1, /device:TPU:29, one launch (start us, length us, event | category | flops | bytes accessed | tf_op | source)
XLA Modules:
  0.0 101.5 jit_solution(2157489811946768981)
XLA Ops:
  0.0 99.2 %shard_map.64 = bf16[2,256,1024]{2,1,0:T(8,128)(2,1)} custom-call(bf16[2,64,1024]{2,1,0:T(8,128)(2,1)} %mem_hbm.1, bf16[2,256,1024]{2,1,0:T(8,128)(2,1)} %bitcast.13, f32[1,4096]{1,0:T(1,128)} %gain_ref.1, bf16[4096,1024]{1,0:T(8,128)(2,1)} %bitcast.10, bf16[65536,128]{1,0:T(8,128)(2,1)} %bitcast.9, bf16[1024,4096]{1,0:T(8,128)(2,1)} %bitcast.11), custom_call_target="tpu_custom_call" | custom-call | tf_op jit(solution)/shard_map/pallas_call | solution.py:485
  99.2 2.3 %copy.9 = bf16[1,2,256,1024]{3,2,1,0:T(8,128)(2,1)} copy(bf16[1,2,256,1024]{3,2,1,0:T(8,128)(2,1)} %bitcast.12) | data formatting | bytes 2097152

commit v2 on v1

--- a/solution.py
+++ b/solution.py
@@ -17,6 +17,7 @@
 SUB = 16
 CHUNK = 256
 SLOTS = 3
+PAIRS = 4
 MESH = pl.DeviceIdType.MESH
 F32 = jnp.float32
 BF16 = jnp.bfloat16
@@ -30,7 +31,7 @@
 def kernel(
     n_pipe, n_tensor,
     mem_hbm, st_hbm, gain_ref, wq_hbm, wkv_hbm, wo_hbm, out_hbm,
-    mem, st, wq, wkv, wo, q, kv, ctx, pd, rd, px, rx, part, staged, squares, done,
+    mem, st, wq, wkv, wo, q, kv, ctx, pd, rd, px, rx, part, staged, squares,
     load_sem, stage_sem, send_sem, recv_ici, recv_d2d, st_ici, st_d2d, pd_sem, px_sem, out_sem,
 ):
     xs, highs = n_tensor // CORES, n_pipe // LOW
@@ -53,12 +54,19 @@
         return (h * LOW + l, xx * CORES + c)
 
     x_peers = [device(hi, lo, turn(x, j, xs), core) for j in range(1, xs)]
-    hi_peers = [device(turn(hi, k, highs), lo, x, core) for k in range(1, highs)]
+    pair = hi + 1 - 2 * lax.rem(hi, 2)
+    inward = highs - 1 - hi
+    inside = jnp.logical_and(hi > 0, hi < highs - 1)
+    pair_peer = device(pair, lo, x, core)
+    inward_peer = device(inward, lo, x, core)
+    hi_sources = [pair, 2 - hi // 2, (highs - 1) * (1 - hi // 2)]
     lo_peer = device(hi, other_lo, x, core)
     sibling = device(hi, lo, x, other_core)
 
-    def block(s, h, far, xx, c):
-        r = pl.multiple_of((far * highs + h) * pos, pos)
+    def block(s, h, far, xx, c, at=None):
+        at = hi if at is None else at
+        near, away = lax.rem(h + at, 2), lax.rem(h // 2 + at // 2, 2)
+        r = pl.multiple_of((away * highs + far * 2 + near) * pos, pos)
         f = pl.multiple_of((xx * CORES + c) * feat, feat)
         return mem.at[s, pl.ds(r, pos), pl.ds(f, feat)]
 
@@ -68,8 +76,9 @@
     def st_block(s, xx, c):
         return st.at[s, :, pl.ds(pl.multiple_of((xx * CORES + c) * feat, feat), feat)]
 
-    counter = [0]
+    counter = [2]
     waits = []
+    traced = [set(), set()]
 
     def remote(src, dst, sem, recv, dev):
         return pltpu.make_async_remote_copy(
@@ -91,40 +100,49 @@
     def like_block():
         return block(0, 0, 0, 0, 0)
 
-    def send_own(s, h, xx, dev, recv):
-        ref = block(s, h, 0, xx, core)
-        send(ref, ref, recv.at[s, slot(h, lo, xx)], dev, like_block)
-
-    def send_low(s, h, xx):
-        send(block(s, h, 0, xx, core), block(s, h, 1, xx, core),
-             recv_ici.at[s, slot(h, lo, xx)], lo_peer, like_block)
-
-    def send_far(s, h, xx):
-        ref = block(s, h, 1, xx, core)
-        send(ref, ref, recv_d2d.at[s, slot(h, other_lo, xx)], sibling, like_block)
-
-    def arrived(s, h, l, xx, recv):
+    def like_blocks(n):
+        return mem.at[:, :n * pos * feat // (seqs * depth), :]
+
+    def send_block(src, dst, recv, dev, sem, *key):
+        traced[sem].add(key)
+        remote(src, dst, sem, recv, dev).start()
+
+    def send_own(s, h, xx, dev, at, sem, *key):
+        send_block(block(s, h, 0, xx, core), block(s, h, 0, xx, core, at),
+                   recv_ici.at[s, slot(h, lo, xx)], dev, sem, "own", s, *key)
+
+    def send_inward(s, h, xx, *key):
+        @pl.when(inside)
+        def _():
+            send_own(s, h, xx, inward_peer, inward, 1, *key)
+
+    def send_low(s, h, xx, *key):
+        send_block(block(s, h, 0, xx, core), block(s, h, 1, xx, core),
+                   recv_ici.at[s, slot(h, lo, xx)], lo_peer, 0, "low", s, *key)
+
+    def send_over(s, h, far, away, xx, *key):
+        ref = block(s, h, far, xx, core)
+        send_block(ref, ref, recv_d2d.at[s, away], sibling, 0, "over", s, far, *key)
+
+    def arrived(s, h, l, xx):
         ref = like_block()
-        remote(ref, ref, 0, recv.at[s, slot(h, l, xx)], sibling).wait_recv()
+        remote(ref, ref, 0, recv_ici.at[s, slot(h, l, xx)], sibling).wait_recv()
 
     st_sends = [[], []]
 
-    def first_send(s):
-        def low():
-            send_low(s, hi, x)
-
-        def across():
-            for dev in x_peers:
-                send_own(s, hi, x, dev, recv_ici)
-
-        def high():
-            for dev in hi_peers:
-                send_own(s, hi, x, dev, recv_ici)
-
-        def over():
-            send_own(s, hi, x, sibling, recv_d2d)
-
-        return low, across, high, over
+    def low_first(s):
+        send_low(s, hi, x, "first")
+
+    def across_first(s):
+        for j, dev in enumerate(x_peers):
+            send_own(s, hi, x, dev, hi, 0, "across", j)
+
+    def high_first(s):
+        send_own(s, hi, x, pair_peer, pair, 0, "first")
+        send_inward(s, hi, x, "first")
+
+    def over_first(s):
+        send_over(s, hi, 0, 0, x, "first")
 
     def state_sends(s):
         ref = st_block(s, x, core)
@@ -135,27 +153,36 @@
     def forward_x(s):
         for j in range(1, xs):
             xx = turn(x, j, xs)
-            arrived(s, hi, lo, xx, recv_ici)
-            send_low(s, hi, xx)
-            for dev in hi_peers:
-                send_own(s, hi, xx, dev, recv_ici)
-            send_own(s, hi, xx, sibling, recv_d2d)
-
-    high_order = [(k, j) for j in range(xs) for k in range(highs - 1, 0, -1)]
-    low_order = [(0, j) for j in range(xs)] + high_order
-
-    def forward_high(s, i):
+            arrived(s, hi, lo, xx)
+            send_own(s, hi, xx, pair_peer, pair, 0, j)
+            send_inward(s, hi, xx, j)
+            send_low(s, hi, xx, j)
+            send_over(s, hi, 0, 0, xx, j)
+
+    high_order = [(0, 0), (0, 1), (1, 0), (1, 1), (2, 0), (2, 1)]
+    low_order = [(None, j) for j in range(xs)] + high_order
+
+    def forward_line(s, i):
         k, j = high_order[i]
-        h, xx = turn(hi, k, highs), turn(x, j, xs)
-        arrived(s, h, lo, xx, recv_ici)
-        send_low(s, h, xx)
-        send_own(s, h, xx, sibling, recv_d2d)
+        h, xx = hi_sources[k], turn(x, j, xs)
+        arrived(s, h, lo, xx)
+        send_own(s, h, xx, inward_peer if k == 0 else pair_peer, inward if k == 0 else pair, 1, "high", i)
+
+    def forward_out(s, i):
+        k, j = high_order[i]
+        h, xx = hi_sources[k], turn(x, j, xs)
+        send_low(s, h, xx, "high", i)
+        send_over(s, h, 0, int(k > 0), xx, "high", i)
+
+    def await_high(s, i):
+        k, j = high_order[i]
+        arrived(s, hi_sources[k], lo, turn(x, j, xs))
 
     def forward_low(s, i):
         k, j = low_order[i]
-        h, xx = turn(hi, k, highs), turn(x, j, xs)
-        arrived(s, h, other_lo, xx, recv_ici)
-        send_far(s, h, xx)
+        h, xx = hi if k is None else hi_sources[k], turn(x, j, xs)
+        arrived(s, h, other_lo, xx)
+        send_over(s, h, 1, int(k is not None and k > 0), xx, i)
 
     def forward_states(s):
         for j in range(1, xs):
@@ -171,10 +198,9 @@
         for sem in st_sends[s]:
             sent(st_block(s, x, core), sem)
 
-    def finish_memory(s, far):
-        for h in range(highs):
-            for xx in range(xs):
-                arrived(s, h, other_lo if far else lo, xx, recv_d2d)
+    def finish_memory(s, away):
+        ref = mem.at[s, :highs * pos, :xs * feat]
+        remote(ref, ref, 0, recv_d2d.at[s, away], sibling).wait_recv()
 
     def steps(n, body, plan=()):
         plan = dict(plan)
@@ -185,14 +211,17 @@
             for t, events in plan.items():
                 @pl.when(i == t)
                 def _(events=events):
-                    for fn, *args in events:
-                        fn(*args)
+                    do(*events)
 
             body(i)
 
     def do(*events):
         for fn, *args in events:
-            fn(*args)
+            if fn.__name__ in ("mid", "tip"):
+                fn(*args)
+            else:
+                with scope("_".join([fn.__name__] + [str(a) for a in args])):
+                    fn(*args)
 
     def normalize(s):
         part[s] = st[s, :, pl.ds(pl.multiple_of(tensor * feat, feat), feat)].astype(F32)
@@ -231,88 +260,86 @@
 
         steps(2 * inner // WIDE, body, plan)
 
-    PAIRS = 2
-
     def attention(s, plan):
         lane = lax.broadcasted_iota(jnp.int32, (1, 2 * HEAD_DIM), 1)
         first = lane < HEAD_DIM
 
         def body(step):
-            for u in range(PAIRS):
-                i = step * PAIRS + u
-                cols = pl.ds(pl.multiple_of(i * 2 * HEAD_DIM, 2 * HEAD_DIM), 2 * HEAD_DIM)
-                vcols = pl.ds(pl.multiple_of(inner + i * 2 * HEAD_DIM, 2 * HEAD_DIM), 2 * HEAD_DIM)
-                qp, kp, vp = q[s, :, cols], kv[:, cols], kv[:, vcols]
-                outs = []
+            places = [pl.multiple_of((step * PAIRS + u) * 2 * HEAD_DIM, 2 * HEAD_DIM) for u in range(PAIRS)]
+            scores, probs = [], []
+            for c in places:
+                qp, kp = q[s, :, pl.ds(c, 2 * HEAD_DIM)], kv[:, pl.ds(c, 2 * HEAD_DIM)]
                 for mine in (first, jnp.logical_not(first)):
                     qh = jnp.where(mine, qp, jnp.zeros_like(qp))
-                    vh = jnp.where(mine, vp, jnp.ones_like(vp))
-                    scores = lax.dot_general(
+                    scores.append(lax.dot_general(
                         qh, kp, (((1,), (1,)), ((), ())), preferred_element_type=F32
-                    )
-                    top = jnp.max(scores, axis=-1, keepdims=True)
-                    probs = jnp.exp(scores - top).astype(BF16)
-                    outs.append(jnp.dot(probs, vh, preferred_element_type=F32))
-                total = jnp.where(first, outs[0], outs[1])
-                sums = pltpu.roll(jnp.where(first, outs[1], outs[0]), HEAD_DIM, 1)
-                ctx[:, cols] = (total / sums).astype(BF16)
+                    ))
+            for one in scores:
+                top = jnp.max(one, axis=-1, keepdims=True)
+                probs.append(jnp.exp(one - top).astype(BF16))
+            for u, c in enumerate(places):
+                vp = kv[:, pl.ds(inner + c, 2 * HEAD_DIM)]
+                both = jnp.concatenate([vp, jnp.ones_like(vp)], axis=1)
+                outs = [jnp.dot(probs[2 * u + e], both, preferred_element_type=F32) for e in range(2)]
+                total = jnp.where(first, outs[0][:, :2 * HEAD_DIM], outs[1][:, :2 * HEAD_DIM])
+                sums = jnp.where(first, outs[0][:, 2 * HEAD_DIM:], outs[1][:, 2 * HEAD_DIM:])
+                ctx[:, pl.ds(c, 2 * HEAD_DIM)] = (total / sums).astype(BF16)
 
         steps(inner // (2 * HEAD_DIM * PAIRS), body, plan)
 
-    width = min(WIDE, feat)
-    tiles = feat // width
-
-    def product(t, i):
-        cols = pl.ds(pl.multiple_of(t * feat + i * width, width), width)
+    cuts = [slice(i, i + min(WIDE, feat)) for i in range(0, feat, min(WIDE, feat))]
+
+    pieces = [slice(i, i + min(TILE, feat)) for i in range(0, feat, min(TILE, feat))]
+
+    def product(t, c):
+        cols = pl.ds(pl.multiple_of(t * feat + c.start, LANES), c.stop - c.start)
         return jnp.dot(ctx[...], wo[:, cols], preferred_element_type=F32)
 
     def output(s):
         order = [turn(x, j, xs) for j in range(1, xs)] + [x]
-
-        def over(j, i):
-            c = slice(i * width, (i + 1) * width)
-            pd[s, j, :, c] = product(order[j] * CORES + other_core, i).astype(BF16)
-            send(pd.at[s, j, :, c], rd.at[s, j, :, c], pd_sem.at[s, j, i], sibling,
-                 lambda: pd.at[0, 0, :, :width])
-
-        def back(j, i):
-            c = slice(i * width, (i + 1) * width)
-            remote(pd.at[s, j, :, c], rd.at[s, j, :, c], 0, pd_sem.at[s, j, i], sibling).wait_recv()
-
-        for j in range(xs - 1):
-            for i in range(tiles):
-                over(j, i)
-            for i in range(tiles):
-                c = slice(i * width, (i + 1) * width)
-                mine = product(order[j] * CORES + core, i)
-                back(j, i)
-                px[s, j, :, c] = (mine + rd[s, j, :, c].astype(F32)).astype(BF16)
+        last = xs - 1
+
+        def over(j):
+            for c in cuts:
+                pd[s, j, :, c] = product(order[j] * CORES + other_core, c).astype(BF16)
+
+        def over_send(j):
+            send(pd.at[s, j], rd.at[s, j], pd_sem.at[s, j], sibling, lambda: pd.at[0, 0])
+
+        def back(j):
+            remote(pd.at[s, j], rd.at[s, j], 0, pd_sem.at[s, j], sibling).wait_recv()
+
+        for j in range(last):
+            over(j)
+            over_send(j)
+            for c in cuts:
+                px[s, j, :, c] = product(order[j] * CORES + core, c).astype(BF16)
+            if s < seqs - 1:
+                over(last)
+            back(j)
+            for i, c in enumerate(pieces):
+                px[s, j, :, c] = (px[s, j, :, c].astype(F32) + rd[s, j, :, c].astype(F32)).astype(BF16)
                 send(px.at[s, j, :, c], rx.at[s, j, :, c], px_sem.at[s, j, i], x_peers[j],
-                     lambda: pd.at[0, 0, :, :width])
-        j = xs - 1
-        for i in range(tiles):
-            over(j, i)
-        for i in range(tiles):
-            c = slice(i * width, (i + 1) * width)
-            part[s, :, c] += product(tensor, i)
-        for i in range(tiles):
-            c = slice(i * width, (i + 1) * width)
-            back(j, i)
-            part[s, :, c] += rd[s, j, :, c].astype(F32)
-
-    def out_copy(s, i):
-        c = slice(i * width, (i + 1) * width)
-        return pltpu.make_async_copy(done.at[s, :, c], out_hbm.at[s, :, c], out_sem.at[s, i])
+                     lambda c=c: pd.at[0, 0, :, c])
+        if s == seqs - 1:
+            over(last)
+        over_send(last)
+        for c in cuts:
+            part[s, :, c] += product(tensor, c)
+        back(last)
+        part[s] += rd[s, last].astype(F32)
+
+    def out_copy(s, i, c):
+        return pltpu.make_async_copy(q.at[s, :, c], out_hbm.at[s, :, c], out_sem.at[s, i])
 
     def finish(s):
-        for i in range(tiles):
-            c = slice(i * width, (i + 1) * width)
+        for i, c in enumerate(pieces):
             total = part[s, :, c]
             for j in range(xs - 1):
                 remote(px.at[s, j, :, c], rx.at[s, j, :, c], 0, px_sem.at[s, j, i], sibling).wait_recv()
                 total += rx[s, j, :, c].astype(F32)
-            done[s, :, c] = total.astype(BF16)
-            out_copy(s, i).start()
+            q[s, :, c] = total.astype(BF16)
+            out_copy(s, i, c).start()
 
     groups = 2 * inner // LANES
     size = CHUNK * groups
@@ -364,55 +391,80 @@
     for copy in loads:
         copy.start()
     barrier = pltpu.get_barrier_semaphore()
-    peers = x_peers + hi_peers + [lo_peer, sibling]
+    peers = x_peers + [pair_peer, lo_peer, sibling]
     for peer in peers:
         pl.semaphore_signal(barrier, inc=1, device_id=peer, device_id_type=MESH)
+
+    @pl.when(inside)
+    def _():
+        pl.semaphore_signal(barrier, inc=1, device_id=inward_peer, device_id_type=MESH)
+
     for i in range(slots):
         stage(i, i).start()
-    for copy in weights:
-        copy.start()
     with scope("barrier"):
-        pl.semaphore_wait(barrier, len(peers))
+        pl.semaphore_wait(barrier, len(peers) + lax.rem(hi + hi // 2, 2))
     with scope("load0"):
         loads[0].wait()
-    low, across, high, over = first_send(0)
-    across(), low(), high(), over()
+    across_first(0)
+    low_first(0)
+    high_first(0)
+    over_first(0)
     with scope("load1"):
         loads[1].wait()
     state_sends(0)
     loads[2].wait()
+    low_first(1)
+    high_first(1)
+    across_first(1)
+    over_first(1)
     loads[3].wait()
-    low1, across1, high1, over1 = first_send(1)
-
-    def second_start():
-        high1()
-        across1()
-        over1()
-        state_sends(1)
+    state_sends(1)
+
+    outside = jnp.logical_not(inside)
+
+    def load(i): weights[i].start()
 
     def fx(s): forward_x(s)
-    def fh(s, i): forward_high(s, i)
+
     def fl(s, i): forward_low(s, i)
+
+    def mid(*events):
+        @pl.when(inside)
+        def _():
+            do(*events)
+
+    def tip(*events):
+        @pl.when(outside)
+        def _():
+            do(*events)
+
+    def ml(s, i): forward_line(s, i)
+
+    def fo(s, i): forward_out(s, i)
+
+    def fi(s, i):
+        forward_line(s, i)
+        forward_out(s, i)
+
+    def ft(s, i):
+        await_high(s, i)
+        forward_out(s, i)
 
     with scope("spread"):
         spread({
-            8: [(fx, 0), (second_start,)],
-            9: [(fl, 0, 0)],
-            10: [(fh, 0, 0)],
-            12: [(fh, 0, 1)],
-            14: [(fl, 0, 1)],
+            6: [(fx, 0), (fl, 0, 0), (mid, (fi, 0, 0), (ml, 0, 2)), (tip, (ft, 0, 0))],
+            10: [(load, 0)],
+            12: [(fl, 0, 1), (mid, (fi, 0, 1), (fo, 0, 2), (fi, 0, 3)), (tip, (ft, 0, 1))],
         })
-    with scope("fh02"):
-        fh(0, 2)
-    with scope("fl02"):
-        fl(0, 2)
-    with scope("fh03"):
-        fh(0, 3)
-    low1()
-    with scope("fl03"):
-        fl(0, 3)
-    with scope("fst0"):
-        forward_states(0)
+    do((load, 1), (mid, (fi, 0, 4)), (tip, (ft, 0, 2)), (fl, 0, 2), (mid, (fi, 0, 5)), (tip, (ft, 0, 3)), (fl, 0, 3))
+    with scope("finmem00"):
+        finish_memory(0, 0)
+    with scope("kv00"):
+        keyvalue(0, 0, {
+            0: [(forward_states, 0)],
+            1: [(tip, (ft, 0, 4)), (fl, 0, 4)],
+            3: [(tip, (ft, 0, 5)), (fx, 1), (fl, 0, 5)],
+        })
     with scope("finst0"):
         finish_states(0)
     with scope("norm0"):
@@ -420,28 +472,37 @@
     with scope("wq"):
         weights[0].wait()
     with scope("query0"):
-        query(0, {0: [(fh, 0, 4)], 1: [(fl, 0, 4)], 2: [(fh, 0, 5)], 3: [(fl, 0, 5)]})
-    with scope("finmem00"):
-        finish_memory(0, 0)
-    with scope("kv00"):
-        keyvalue(0, 0, {0: [(fx, 1)], 1: [(fl, 0, 6)], 2: [(fh, 1, 0)], 3: [(fl, 0, 7)]})
+        query(0, {
+            1: [(fl, 0, 6)],
+            2: [(mid, (fi, 1, 0), (ml, 1, 2)), (tip, (ft, 1, 0))],
+        })
+    do((mid, (fi, 1, 1), (fo, 1, 2), (fi, 1, 3)), (tip, (ft, 1, 1)), (fl, 0, 7))
     with scope("finmem01"):
         finish_memory(0, 1)
     with scope("kv01"):
-        keyvalue(0, 1, {0: [(fh, 1, 1)], 1: [(fl, 1, 0)], 2: [(fh, 1, 2)], 3: [(fl, 1, 1)]})
+        keyvalue(0, 1, {
+            1: [(fl, 1, 0), (tip, (ft, 1, 2)), (mid, (fi, 1, 4))],
+            2: [(forward_states, 1)],
+            3: [(fl, 1, 1), (mid, (fi, 1, 5)), (tip, (ft, 1, 3))],
+        })
     with scope("att0"):
-        attention(0, {0: [(fh, 1, 3)], 1: [(fl, 1, 2)], 2: [(fh, 1, 4), (forward_states, 1)], 3: [(fl, 1, 3)]})
-    with scope("fh15"):
-        fh(1, 5)
+        attention(0, {
+            0: [(fl, 1, 2)],
+            1: [(tip, (ft, 1, 4))],
+        })
     with scope("finst1"):
         finish_states(1)
     with scope("norm1"):
         normalize(1)
     with scope("query1"):
-        query(1, {1: [(fl, 1, 4)], 3: [(fl, 1, 5)]})
+        query(1, {
+            0: [(fl, 1, 3), (tip, (ft, 1, 5))],
+            2: [(fl, 1, 4)],
+        })
     weights[1].wait()
     with scope("output0"):
         output(0)
+    do((fl, 1, 5))
     with scope("finmem10"):
         finish_memory(1, 0)
     with scope("kv10"):
@@ -450,20 +511,26 @@
         finish_memory(1, 1)
     with scope("kv11"):
         keyvalue(1, 1, {})
-    with scope("finish0"):
-        finish(0)
     with scope("att1"):
         attention(1, {})
     with scope("output1"):
         output(1)
+    with scope("finish0"):
+        finish(0)
     with scope("finish1"):
         finish(1)
+    assert [len(t) for t in traced] == [54, 16], [len(t) for t in traced]
     with scope("end"):
         for like, sem in waits:
             sent(like(), sem)
         for s in range(seqs):
-            for i in range(tiles):
-                out_copy(s, i).wait()
+            for i, c in enumerate(pieces):
+                out_copy(s, i, c).wait()
+        sent(like_blocks(len(traced[0])), 0)
+
+        @pl.when(inside)
+        def _():
+            sent(like_blocks(len(traced[1])), 1)
 
 
 def fused(n_pipe, n_tensor, memory, states, norm_gain, w_query, w_keyvalue, w_output):
@@ -476,9 +543,8 @@
     weight_kv = w_keyvalue[0].reshape(depth, 2, inner // LANES, LANES)
     weight_kv = weight_kv.transpose(0, 2, 1, 3).reshape(depth * groups, LANES)
     blocks = n_pipe * xs
-    tiles = feat // min(WIDE, feat)
-    per_seq = ((xs - 1) + (highs - 1) + 2 + (xs - 1) * (highs + 1) + 2 * (highs - 1) * xs
-               + highs * xs + 2 * xs + 2 * xs * tiles)
+    tiles = feat // min(TILE, feat)
+    copies = seqs * (xs + xs + xs + (xs - 1) * tiles) + 2
     any_space = pl.BlockSpec(memory_space=pl.ANY)
     in_vmem = pl.BlockSpec(memory_space=pltpu.VMEM)
     dma = pltpu.SemaphoreType.DMA
@@ -493,7 +559,7 @@
             pltpu.VMEM((depth, inner), BF16),
             pltpu.VMEM((depth, 2 * inner), BF16),
             pltpu.VMEM((inner, depth), BF16),
-            pltpu.VMEM((seqs, rows, inner), BF16),
+            pltpu.VMEM((seqs, rows, max(inner, feat)), BF16),
             pltpu.VMEM((enc, 2 * inner), BF16),
             pltpu.VMEM((rows, inner), BF16),
             pltpu.VMEM((seqs, xs, rows, feat), BF16),
@@ -503,20 +569,19 @@
             pltpu.VMEM((seqs, rows, feat), F32),
             pltpu.VMEM((SLOTS, CHUNK * groups, LANES), BF16),
             pltpu.VMEM((rows, LANES), F32),
-            pltpu.VMEM((seqs, rows, feat), BF16),
             dma((6,)),
             dma((SLOTS,)),
-            dma((seqs * per_seq,)),
+            dma((copies,)),
             dma((seqs, blocks)),
-            dma((seqs, blocks)),
+            dma((seqs, LOW)),
             dma((seqs, xs)),
             dma((seqs, xs)),
-            dma((seqs, xs, tiles)),
+            dma((seqs, xs)),
             dma((seqs, xs - 1, tiles)),
             dma((seqs, tiles)),
         ],
         compiler_params=pltpu.CompilerParams(
-            collective_id=0, has_side_effects=True, vmem_limit_bytes=66_000_000
+            collective_id=0, has_side_effects=True, vmem_limit_bytes=67_000_000
         ),
     )(memory, states[0], norm_gain, w_query[0], weight_kv, w_output[0])
     return out[None]
@@ -572,6 +637,8 @@
     out_specs = P("pipe", None, None, "tensor")
     n_pipe, n_tensor = mesh.shape["pipe"], mesh.shape["tensor"]
     even = n_pipe % LOW == 0 and n_tensor % CORES == 0 and n_pipe > LOW and n_tensor > CORES
+    even = even and n_pipe // LOW == 4 and n_tensor // CORES == 2
+    even = even and n_pipe // LOW == 4 and n_tensor // CORES == 2
     body = per_device
     if even and copies_per_sequence(n_pipe, n_tensor) <= MAX_COPIES:
         body = functools.partial(fused, n_pipe, n_tensor)

time: 102 us -> 85.6 us (0.84)
  the two profiles are of different devices: /device:TPU:29 before, /device:TPU:0 now
where the time goes in v2:
time: 85.6 us; the launch traced here: 85.3 us
  Pallas kernels  83.1 us (97%)
  local copies, waits for them, and re-layouts  2.26 us (3%)
    pallas_call x1, Pallas kernels, fused(): pl.pallas_call(functools.partial(kernel, n_pipe, n_tensor), out_shape=jax...  83.1 us
    unnamed x1, local copies, waits for them, and re-layouts  2.26 us

profile of v2, /device:TPU:0, one launch (start us, length us, event | category | flops | bytes accessed | tf_op | source)
XLA Modules:
  0.0 85.3 jit_solution(5212834826010202098)
XLA Ops:
  0.0 83.1 %shard_map.64 = bf16[2,256,1024]{2,1,0:T(8,128)(2,1)} custom-call(bf16[2,64,1024]{2,1,0:T(8,128)(2,1)} %mem_hbm.1, bf16[2,256,1024]{2,1,0:T(8,128)(2,1)} %bitcast.13, f32[1,4096]{1,0:T(1,128)} %gain_ref.1, bf16[4096,1024]{1,0:T(8,128)(2,1)} %bitcast.10, bf16[65536,128]{1,0:T(8,128)(2,1)} %bitcast.9, bf16[1024,4096]{1,0:T(8,128)(2,1)} %bitcast.11), custom_call_target="tpu_custom_call" | custom-call | tf_op jit(solution)/shard_map/pallas_call | solution.py:551
  83.1 2.3 %copy.9 = bf16[1,2,256,1024]{3,2,1,0:T(8,128)(2,1)} copy(bf16[1,2,256,1024]{3,2,1,0:T(8,128)(2,1)} %bitcast.12) | data formatting | bytes 2097152

commit v3 on v2

--- a/solution.py
+++ b/solution.py
@@ -31,7 +31,7 @@
 def kernel(
     n_pipe, n_tensor,
     mem_hbm, st_hbm, gain_ref, wq_hbm, wkv_hbm, wo_hbm, out_hbm,
-    mem, st, wq, wkv, wo, q, kv, ctx, pd, rd, px, rx, part, staged, squares,
+    mem, st, wq, wkv, wo, q, kv, pd, rd, px, rx, part, staged, squares,
     load_sem, stage_sem, send_sem, recv_ici, recv_d2d, st_ici, st_d2d, pd_sem, px_sem, out_sem,
 ):
     xs, highs = n_tensor // CORES, n_pipe // LOW
@@ -160,6 +160,7 @@
             send_over(s, hi, 0, 0, xx, j)
 
     high_order = [(0, 0), (0, 1), (1, 0), (1, 1), (2, 0), (2, 1)]
+    SIDEWAYS = 3
     low_order = [(None, j) for j in range(xs)] + high_order
 
     def forward_line(s, i):
@@ -171,7 +172,8 @@
     def forward_out(s, i):
         k, j = high_order[i]
         h, xx = hi_sources[k], turn(x, j, xs)
-        send_low(s, h, xx, "high", i)
+        if (s, i) != (seqs - 1, SIDEWAYS):
+            send_low(s, h, xx, "high", i)
         send_over(s, h, 0, int(k > 0), xx, "high", i)
 
     def await_high(s, i):
@@ -182,6 +184,9 @@
         k, j = low_order[i]
         h, xx = hi if k is None else hi_sources[k], turn(x, j, xs)
         arrived(s, h, other_lo, xx)
+        if s == seqs - 1 and k == high_order[SIDEWAYS][0] and j == 0:
+            ref = block(s, h, 1, xx, core)
+            send_block(ref, ref, recv_ici.at[s, slot(h, other_lo, xx)], x_peers[0], 0, "sideways", s)
         send_over(s, h, 1, int(k is not None and k > 0), xx, i)
 
     def forward_states(s):
@@ -192,7 +197,8 @@
             st_sends[s].append(send(ref, ref, st_d2d.at[s, xx], sibling, None, False))
 
     def finish_states(s):
-        for xx in range(xs):
+        for j in range(int(s == seqs - 1), xs):
+            xx = turn(x, j, xs)
             ref = st_block(s, xx, other_core)
             remote(ref, ref, 0, st_d2d.at[s, xx], sibling).wait_recv()
         for sem in st_sends[s]:
@@ -222,6 +228,11 @@
             else:
                 with scope("_".join([fn.__name__] + [str(a) for a in args])):
                     fn(*args)
+
+    def set_scale(s):
+        mean = jnp.sum(squares[s], axis=-1, keepdims=True) * (1.0 / depth)
+        scale = lax.rsqrt(mean + 1e-06) * (HEAD_DIM ** -0.5)
+        squares[s] = jnp.broadcast_to(scale, (rows, LANES))
 
     def normalize(s):
         part[s] = st[s, :, pl.ds(pl.multiple_of(tensor * feat, feat), feat)].astype(F32)
@@ -235,30 +246,83 @@
                 xf = st[s, some, cols].astype(F32)
                 total += xf * xf
                 st[s, some, cols] = (xf * gain_ref[:, cols]).astype(BF16)
-            squares[some, :] = total
-
-        mean = jnp.sum(squares[...], axis=-1, keepdims=True) * (1.0 / depth)
-        scale = lax.rsqrt(mean + 1e-06) * (HEAD_DIM ** -0.5)
-        squares[...] = jnp.broadcast_to(scale, squares.shape)
+            squares[s, some, :] = total
+
+        set_scale(s)
 
     def query(s, plan):
         def body(i):
             cols = pl.ds(pl.multiple_of(i * TILE, TILE), TILE)
             full = jnp.dot(st[s], wq[:, cols], preferred_element_type=F32)
-            scale = squares[...]
+            scale = squares[s]
             q[s, :, cols] = (full * jnp.concatenate([scale] * (TILE // LANES), axis=1)).astype(BF16)
 
         steps(inner // TILE, body, plan)
 
-    half = highs * pos
-
-    def keyvalue(s, far, plan):
+    def chip_features(xx, c):
+        return pl.multiple_of((xx * CORES + c) * feat, feat)
+
+    def early_query(s, plan):
+        ref = st_block(s, x, other_core)
+        remote(ref, ref, 0, st_d2d.at[s, x], sibling).wait_recv()
+
+        @pl.loop(0, rows // SUB)
+        def _(i):
+            some = pl.ds(pl.multiple_of(i * SUB, SUB), SUB)
+            total = jnp.zeros((SUB, LANES), F32)
+            for c in range(CORES):
+                for g in range(feat // LANES):
+                    cols = pl.ds(pl.multiple_of(chip_features(x, c) + g * LANES, LANES), LANES)
+                    xf = st[s, some, cols].astype(F32)
+                    total += xf * xf
+                    pd[s, c, some, g * LANES:(g + 1) * LANES] = (xf * gain_ref[:, cols]).astype(BF16)
+            squares[s, some, :] = total
+
         def body(i):
             cols = pl.ds(pl.multiple_of(i * WIDE, WIDE), WIDE)
-            full = jnp.dot(mem[s, far * half:(far + 1) * half], wkv[:, cols], preferred_element_type=F32)
-            kv[far * half:(far + 1) * half, cols] = full.astype(BF16)
-
-        steps(2 * inner // WIDE, body, plan)
+            part[s, :, cols] = sum(
+                jnp.dot(pd[s, c], wq[pl.ds(chip_features(x, c), feat), cols], preferred_element_type=F32)
+                for c in range(CORES)
+            )
+
+        steps(inner // WIDE, body, plan)
+
+    def late_query(s, plan):
+        xx = turn(x, 1, xs)
+
+        @pl.loop(0, rows // SUB)
+        def _(i):
+            some = pl.ds(pl.multiple_of(i * SUB, SUB), SUB)
+            total = squares[s, some, :]
+            for c in range(CORES):
+                for g in range(feat // LANES):
+                    cols = pl.ds(pl.multiple_of(chip_features(xx, c) + g * LANES, LANES), LANES)
+                    xf = st[s, some, cols].astype(F32)
+                    total += xf * xf
+                    st[s, some, cols] = (xf * gain_ref[:, cols]).astype(BF16)
+            squares[s, some, :] = total
+
+        set_scale(s)
+
+        def body(i):
+            cols = pl.ds(pl.multiple_of(i * WIDE, WIDE), WIDE)
+            mine = pl.ds(chip_features(xx, 0), CORES * feat)
+            full = part[s, :, cols] + jnp.dot(st[s, :, mine], wq[mine, cols], preferred_element_type=F32)
+            q[s, :, cols] = (full * jnp.concatenate([squares[s]] * (WIDE // LANES), axis=1)).astype(BF16)
+
+        steps(inner // WIDE, body, plan)
+        part[s] = st[s, :, pl.ds(pl.multiple_of(tensor * feat, feat), feat)].astype(F32)
+
+    half = highs * pos
+
+    def keyvalue(s, far, plan, per=1):
+        def body(i):
+            for u in range(per):
+                cols = pl.ds(pl.multiple_of((i * per + u) * WIDE, WIDE), WIDE)
+                full = jnp.dot(mem[s, far * half:(far + 1) * half], wkv[:, cols], preferred_element_type=F32)
+                kv[far * half:(far + 1) * half, cols] = full.astype(BF16)
+
+        steps(2 * inner // (WIDE * per), body, plan)
 
     def attention(s, plan):
         lane = lax.broadcasted_iota(jnp.int32, (1, 2 * HEAD_DIM), 1)
@@ -283,7 +347,7 @@
                 outs = [jnp.dot(probs[2 * u + e], both, preferred_element_type=F32) for e in range(2)]
                 total = jnp.where(first, outs[0][:, :2 * HEAD_DIM], outs[1][:, :2 * HEAD_DIM])
                 sums = jnp.where(first, outs[0][:, 2 * HEAD_DIM:], outs[1][:, 2 * HEAD_DIM:])
-                ctx[:, pl.ds(c, 2 * HEAD_DIM)] = (total / sums).astype(BF16)
+                q[s, :, pl.ds(c, 2 * HEAD_DIM)] = (total / sums).astype(BF16)
 
         steps(inner // (2 * HEAD_DIM * PAIRS), body, plan)
 
@@ -291,48 +355,72 @@
 
     pieces = [slice(i, i + min(TILE, feat)) for i in range(0, feat, min(TILE, feat))]
 
-    def product(t, c):
+    def product(s, t, c):
         cols = pl.ds(pl.multiple_of(t * feat + c.start, LANES), c.stop - c.start)
-        return jnp.dot(ctx[...], wo[:, cols], preferred_element_type=F32)
+        return jnp.dot(q[s, :, :inner], wo[:, cols], preferred_element_type=F32)
+
+    order = [turn(x, j, xs) for j in range(1, xs)] + [x]
+    last = xs - 1
+    whole = slice(0, feat)
+    lead, rest = [pieces[0]], [slice(pieces[1].start, cuts[0].stop)] + cuts[1:]
+
+    def bounds(group):
+        return slice(group[0].start, group[-1].stop)
+
+    def over(s, j, group):
+        for c in group:
+            pd[s, j, :, c] = product(s, order[j] * CORES + other_core, c).astype(BF16)
+
+    def mine(s, j, group):
+        for c in group:
+            px[s, j, :, c] = product(s, order[j] * CORES + core, c).astype(BF16)
+
+    def over_send(s, j, g, c):
+        send(pd.at[s, j, :, c], rd.at[s, j, :, c], pd_sem.at[s, j, g], sibling, lambda: pd.at[0, 0, :, c])
+
+    def back(s, j, g, c):
+        remote(pd.at[s, j, :, c], rd.at[s, j, :, c], 0, pd_sem.at[s, j, g], sibling).wait_recv()
+
+    def pass_on(s, g, b):
+        for j in range(last):
+            back(s, j, g, b)
+            for i, c in enumerate(pieces):
+                if b.start <= c.start < b.stop:
+                    px[s, j, :, c] = (px[s, j, :, c].astype(F32) + rd[s, j, :, c].astype(F32)).astype(BF16)
+                    send(px.at[s, j, :, c], rx.at[s, j, :, c], px_sem.at[s, j, i], x_peers[j],
+                         lambda c=c: pd.at[0, 0, :, c])
 
     def output(s):
-        order = [turn(x, j, xs) for j in range(1, xs)] + [x]
-        last = xs - 1
-
-        def over(j):
-            for c in cuts:
-                pd[s, j, :, c] = product(order[j] * CORES + other_core, c).astype(BF16)
-
-        def over_send(j):
-            send(pd.at[s, j], rd.at[s, j], pd_sem.at[s, j], sibling, lambda: pd.at[0, 0])
-
-        def back(j):
-            remote(pd.at[s, j], rd.at[s, j], 0, pd_sem.at[s, j], sibling).wait_recv()
-
         for j in range(last):
-            over(j)
-            over_send(j)
-            for c in cuts:
-                px[s, j, :, c] = product(order[j] * CORES + core, c).astype(BF16)
-            if s < seqs - 1:
-                over(last)
-            back(j)
-            for i, c in enumerate(pieces):
-                px[s, j, :, c] = (px[s, j, :, c].astype(F32) + rd[s, j, :, c].astype(F32)).astype(BF16)
-                send(px.at[s, j, :, c], rx.at[s, j, :, c], px_sem.at[s, j, i], x_peers[j],
-                     lambda c=c: pd.at[0, 0, :, c])
-        if s == seqs - 1:
-            over(last)
-        over_send(last)
+            over(s, j, cuts)
+            mine(s, j, cuts)
+            over_send(s, j, 0, whole)
+
+    def output_early(s):
+        for j in range(last):
+            over(s, j, lead)
+            over_send(s, j, 0, bounds(lead))
+            mine(s, j, lead)
+            over(s, j, rest)
+            over_send(s, j, 1, bounds(rest))
+        pass_on(s, 0, bounds(lead))
+        for j in range(last):
+            mine(s, j, rest)
+        pass_on(s, 1, bounds(rest))
+
+    def output_here(s):
+        over(s, last, cuts)
+        over_send(s, last, 0, whole)
         for c in cuts:
-            part[s, :, c] += product(tensor, c)
-        back(last)
-        part[s] += rd[s, last].astype(F32)
+            part[s, :, c] += product(s, tensor, c)
 
     def out_copy(s, i, c):
         return pltpu.make_async_copy(q.at[s, :, c], out_hbm.at[s, :, c], out_sem.at[s, i])
 
     def finish(s):
+        back(s, last, 0, whole)
+        for i, c in enumerate(pieces):
+            part[s, :, c] += rd[s, last, :, c].astype(F32)
         for i, c in enumerate(pieces):
             total = part[s, :, c]
             for j in range(xs - 1):
@@ -424,6 +512,8 @@
 
     def load(i): weights[i].start()
 
+    def across(s): pass_on(s, 0, whole)
+
     def fx(s): forward_x(s)
 
     def fl(s, i): forward_low(s, i)
@@ -456,21 +546,23 @@
             10: [(load, 0)],
             12: [(fl, 0, 1), (mid, (fi, 0, 1), (fo, 0, 2), (fi, 0, 3)), (tip, (ft, 0, 1))],
         })
-    do((load, 1), (mid, (fi, 0, 4)), (tip, (ft, 0, 2)), (fl, 0, 2), (mid, (fi, 0, 5)), (tip, (ft, 0, 3)), (fl, 0, 3))
+    do((load, 1), (mid, (fi, 0, 4)), (tip, (ft, 0, 2)), (fl, 0, 2))
+    weights[0].wait()
+    with scope("early"):
+        early_query(1, {1: [(mid, (fi, 0, 5))]})
+    do((fl, 0, 3), (tip, (ft, 0, 3)))
     with scope("finmem00"):
         finish_memory(0, 0)
     with scope("kv00"):
         keyvalue(0, 0, {
             0: [(forward_states, 0)],
             1: [(tip, (ft, 0, 4)), (fl, 0, 4)],
-            3: [(tip, (ft, 0, 5)), (fx, 1), (fl, 0, 5)],
-        })
+        }, 2)
+    do((tip, (ft, 0, 5)), (fx, 1), (fl, 0, 5))
     with scope("finst0"):
         finish_states(0)
     with scope("norm0"):
         normalize(0)
-    with scope("wq"):
-        weights[0].wait()
     with scope("query0"):
         query(0, {
             1: [(fl, 0, 6)],
@@ -482,39 +574,40 @@
     with scope("kv01"):
         keyvalue(0, 1, {
             1: [(fl, 1, 0), (tip, (ft, 1, 2)), (mid, (fi, 1, 4))],
-            2: [(forward_states, 1)],
-            3: [(fl, 1, 1), (mid, (fi, 1, 5)), (tip, (ft, 1, 3))],
-        })
+        }, 2)
+    do((forward_states, 1), (fl, 1, 1))
     with scope("att0"):
         attention(0, {
-            0: [(fl, 1, 2)],
-            1: [(tip, (ft, 1, 4))],
+            0: [(mid, (fi, 1, 5)), (tip, (ft, 1, 3)), (fl, 1, 2)],
         })
     with scope("finst1"):
         finish_states(1)
-    with scope("norm1"):
-        normalize(1)
     with scope("query1"):
-        query(1, {
-            0: [(fl, 1, 3), (tip, (ft, 1, 5))],
-            2: [(fl, 1, 4)],
+        late_query(1, {
+            0: [(tip, (ft, 1, 4)), (fl, 1, 3)],
+            1: [(tip, (ft, 1, 5))],
         })
     weights[1].wait()
+    do((fl, 1, 4))
     with scope("output0"):
         output(0)
-    do((fl, 1, 5))
     with scope("finmem10"):
         finish_memory(1, 0)
     with scope("kv10"):
-        keyvalue(1, 0, {1: [(fl, 1, 6)], 3: [(fl, 1, 7)]})
+        keyvalue(1, 0, {1: [(across, 0), (fl, 1, 6)]}, 2)
+    do((fl, 1, 5), (fl, 1, 7))
     with scope("finmem11"):
         finish_memory(1, 1)
     with scope("kv11"):
-        keyvalue(1, 1, {})
+        keyvalue(1, 1, {}, 2)
     with scope("att1"):
         attention(1, {})
     with scope("output1"):
-        output(1)
+        output_early(1)
+    with scope("here0"):
+        output_here(0)
+    with scope("here1"):
+        output_here(1)
     with scope("finish0"):
         finish(0)
     with scope("finish1"):
@@ -544,7 +637,7 @@
     weight_kv = weight_kv.transpose(0, 2, 1, 3).reshape(depth * groups, LANES)
     blocks = n_pipe * xs
     tiles = feat // min(TILE, feat)
-    copies = seqs * (xs + xs + xs + (xs - 1) * tiles) + 2
+    copies = seqs * (xs + xs + 2 * xs + (xs - 1) * tiles) + 2
     any_space = pl.BlockSpec(memory_space=pl.ANY)
     in_vmem = pl.BlockSpec(memory_space=pltpu.VMEM)
     dma = pltpu.SemaphoreType.DMA
@@ -561,14 +654,13 @@
             pltpu.VMEM((inner, depth), BF16),
             pltpu.VMEM((seqs, rows, max(inner, feat)), BF16),
             pltpu.VMEM((enc, 2 * inner), BF16),
-            pltpu.VMEM((rows, inner), BF16),
             pltpu.VMEM((seqs, xs, rows, feat), BF16),
             pltpu.VMEM((seqs, xs, rows, feat), BF16),
             pltpu.VMEM((seqs, xs - 1, rows, feat), BF16),
             pltpu.VMEM((seqs, xs - 1, rows, feat), BF16),
             pltpu.VMEM((seqs, rows, feat), F32),
             pltpu.VMEM((SLOTS, CHUNK * groups, LANES), BF16),
-            pltpu.VMEM((rows, LANES), F32),
+            pltpu.VMEM((seqs, rows, LANES), F32),
             dma((6,)),
             dma((SLOTS,)),
             dma((copies,)),
@@ -576,7 +668,7 @@
             dma((seqs, LOW)),
             dma((seqs, xs)),
             dma((seqs, xs)),
-            dma((seqs, xs)),
+            dma((seqs, xs, 2)),
             dma((seqs, xs - 1, tiles)),
             dma((seqs, tiles)),
         ],

time: 85.6 us -> 79.9 us (0.933)
  Pallas kernels: 83.1 us -> 77.4 us
    pallas_call x1, Pallas kernels: 83.1 us -> 77.4 us  [fused(): pl.pallas_call(functools.partial(kernel, n_pipe, n_tensor), out_shape=jax...]
where the time goes in v3:
time: 79.9 us; the launch traced here: 79.6 us
  Pallas kernels  77.4 us (97%)
  local copies, waits for them, and re-layouts  2.26 us (3%)
    pallas_call x1, Pallas kernels, fused(): pl.pallas_call(functools.partial(kernel, n_pipe, n_tensor), out_shape=jax...  77.4 us
    unnamed x1, local copies, waits for them, and re-layouts  2.26 us

profile of v3, /device:TPU:0, one launch (start us, length us, event | category | flops | bytes accessed | tf_op | source)
XLA Modules:
  0.0 79.6 jit_solution(5576170143621994809)
XLA Ops:
  0.0 77.4 %shard_map.64 = bf16[2,256,1024]{2,1,0:T(8,128)(2,1)} custom-call(bf16[2,64,1024]{2,1,0:T(8,128)(2,1)} %mem_hbm.1, bf16[2,256,1024]{2,1,0:T(8,128)(2,1)} %bitcast.13, f32[1,4096]{1,0:T(1,128)} %gain_ref.1, bf16[4096,1024]{1,0:T(8,128)(2,1)} %bitcast.10, bf16[65536,128]{1,0:T(8,128)(2,1)} %bitcast.9, bf16[1024,4096]{1,0:T(8,128)(2,1)} %bitcast.11), custom_call_target="tpu_custom_call" | custom-call | tf_op jit(solution)/shard_map/pallas_call | solution.py:644
  77.4 2.3 %copy.9 = bf16[1,2,256,1024]{3,2,1,0:T(8,128)(2,1)} copy(bf16[1,2,256,1024]{3,2,1,0:T(8,128)(2,1)} %bitcast.12) | data formatting | bytes 2097152

commit v4 on v3

--- a/solution.py
+++ b/solution.py
@@ -160,7 +160,7 @@
             send_over(s, hi, 0, 0, xx, j)
 
     high_order = [(0, 0), (0, 1), (1, 0), (1, 1), (2, 0), (2, 1)]
-    SIDEWAYS = 3
+    SIDEWAYS = (1, 3)
     low_order = [(None, j) for j in range(xs)] + high_order
 
     def forward_line(s, i):
@@ -172,7 +172,7 @@
     def forward_out(s, i):
         k, j = high_order[i]
         h, xx = hi_sources[k], turn(x, j, xs)
-        if (s, i) != (seqs - 1, SIDEWAYS):
+        if not (s == seqs - 1 and i in SIDEWAYS):
             send_low(s, h, xx, "high", i)
         send_over(s, h, 0, int(k > 0), xx, "high", i)
 
@@ -184,9 +184,9 @@
         k, j = low_order[i]
         h, xx = hi if k is None else hi_sources[k], turn(x, j, xs)
         arrived(s, h, other_lo, xx)
-        if s == seqs - 1 and k == high_order[SIDEWAYS][0] and j == 0:
+        if s == seqs - 1 and j == 0 and k in [high_order[i][0] for i in SIDEWAYS]:
             ref = block(s, h, 1, xx, core)
-            send_block(ref, ref, recv_ici.at[s, slot(h, other_lo, xx)], x_peers[0], 0, "sideways", s)
+            send_block(ref, ref, recv_ici.at[s, slot(h, other_lo, xx)], x_peers[0], 0, "sideways", s, k)
         send_over(s, h, 1, int(k is not None and k > 0), xx, i)
 
     def forward_states(s):
@@ -584,11 +584,10 @@
         finish_states(1)
     with scope("query1"):
         late_query(1, {
-            0: [(tip, (ft, 1, 4)), (fl, 1, 3)],
-            1: [(tip, (ft, 1, 5))],
+            0: [(tip, (ft, 1, 4))],
+            1: [(tip, (ft, 1, 5)), (fl, 1, 4), (fl, 1, 3)],
         })
     weights[1].wait()
-    do((fl, 1, 4))
     with scope("output0"):
         output(0)
     with scope("finmem10"):

time: 79.9 us -> 79.9 us (level)
  no operation moved by 1% of the time
where the time goes in v4:
time: 79.9 us; the launch traced here: 79.6 us
  Pallas kernels  77.4 us (97%)
  local copies, waits for them, and re-layouts  2.26 us (3%)
    pallas_call x1, Pallas kernels, fused(): pl.pallas_call(functools.partial(kernel, n_pipe, n_tensor), out_shape=jax...  77.4 us
    unnamed x1, local copies, waits for them, and re-layouts  2.26 us

profile of v4, /device:TPU:0, one launch (start us, length us, event | category | flops | bytes accessed | tf_op | source)
XLA Modules:
  0.0 79.6 jit_solution(17606791813489646555)
XLA Ops:
  0.0 77.4 %shard_map.64 = bf16[2,256,1024]{2,1,0:T(8,128)(2,1)} custom-call(bf16[2,64,1024]{2,1,0:T(8,128)(2,1)} %mem_hbm.1, bf16[2,256,1024]{2,1,0:T(8,128)(2,1)} %bitcast.13, f32[1,4096]{1,0:T(1,128)} %gain_ref.1, bf16[4096,1024]{1,0:T(8,128)(2,1)} %bitcast.10, bf16[65536,128]{1,0:T(8,128)(2,1)} %bitcast.9, bf16[1024,4096]{1,0:T(8,128)(2,1)} %bitcast.11), custom_call_target="tpu_custom_call" | custom-call | tf_op jit(solution)/shard_map/pallas_call | solution.py:643
  77.4 2.3 %copy.9 = bf16[1,2,256,1024]{3,2,1,0:T(8,128)(2,1)} copy(bf16[1,2,256,1024]{3,2,1,0:T(8,128)(2,1)} %bitcast.12) | data formatting | bytes 2097152
